TPU v7x, 32 devices: a 4x4x1 block of a 4x4x8 slice. The times are simulated.
32 devices in a mesh: dp: 1 (over z), tp2: 4 (over y), tp: 8 (over x, core).
Axes of the slice: x: 4, y: 4, z: 1, core: 2. Of those that a mesh axis runs over, the one named last changes fastest.
The devices are a block of a 4x4x8 slice.
Arguments:
- attn_out: bfloat16 [8192, 12288], P('dp', 'tp')
- w_out: bfloat16 [12288, 12288], P('tp', 'tp2')
- residual: bfloat16 [8192, 12288], P(('dp', 'tp'), 'tp2')
- norm_gain: float32 [12288], P('tp2')
Outputs:
- output 1: bfloat16 [8192, 12288], P(('dp', 'tp'), 'tp2')
- output 2: bfloat16 [8192, 12288], P(('dp', 'tp'), 'tp2')
All inputs are finite; a program needn't handle non-finite values.
Results may differ from a plain program's by a relative error of at most 0.00707124.
Values are sent between devices in bfloat16 or wider.
A program may use at most 768 MiB of HBM per device.

v0:
```python
import functools

import jax
import jax.numpy as jnp
from jax import lax
from jax.experimental import pallas as pl
from jax.experimental.pallas import tpu as pltpu
from jax.sharding import PartitionSpec as P

EPS_NORM = 1e-6
MESH = pl.DeviceIdType.MESH
CORES = 2
CN = 256
LAG = 7
FIRST = 8
AHEAD = 6
PIECES = 4


def kernel(ny, chips, a, w, r, hbuf, ssq_out, wbuf, av, wv, ov, lv, rv, ssacc, svr, at, pv, sb, sp, sg,
           al_sem, ap_send, ap_recv, ax_send, ax_recv, ay_send, ay_recv, ao_recv, af_send, af_recv,
           wp_send, wp_recv, wa_send, wa_recv, wf_send, wf_recv, o_send, o_recv,
           wl_sem, r_sem, s_send, s_recv, at_sem, sb_send, sb_recv, sp_send, sp_recv, sf_send, sf_recv):
    rows, cols = r.shape
    last = cols // CN - 1
    quarter = rows // ny
    piece = quarter // PIECES
    tile = min(256, rows)
    me, y = lax.axis_index("tp"), lax.axis_index("tp2")
    x, c = lax.div(me, CORES), lax.rem(me, CORES)
    o = 1 - c
    xa = x + 1 - 2 * lax.rem(x, 2)
    xb = chips - 1 - x
    xab = chips - 1 - xa
    yp, ym = lax.rem(y + 1, ny), lax.rem(y + ny - 1, ny)
    part = {"tp": x * CORES + o}
    acore, aother = {"tp": xa * CORES + c}, {"tp": xa * CORES + o}
    bcore, bother = {"tp": xb * CORES + c}, {"tp": xb * CORES + o}
    up, down = {"tp2": yp}, {"tp2": ym}

    def remote(src, dst, send, recv, device):
        return pltpu.make_async_remote_copy(
            src_ref=src, dst_ref=dst, send_sem=send, recv_sem=recv, device_id=device, device_id_type=MESH)

    def arow(owner, size=None, shift=0):
        return pl.ds(pl.multiple_of(owner * rows + shift, 16), rows if size is None else size)

    def qrow(q, t):
        return pl.ds(pl.multiple_of(q * quarter + t * piece, 16), piece)

    def wcol(j):
        return pl.ds(pl.multiple_of(j * CN, CN), CN)

    own_rows = (xb * CORES + c, me)
    part_rows = (xb * CORES + o, x * CORES + o)

    def a_local(g):
        return pltpu.make_async_copy(a.at[arow(own_rows[g])], av.at[g, 0], al_sem.at[g])

    def a_part(g):
        return remote(a.at[arow(part_rows[g])], av.at[g, 1], ap_send, ap_recv.at[g], part)

    def a_cross(g, s, t):
        core, device = ((c, acore), (o, aother))[s]
        owner = (xab, xa)[g] * CORES + core
        return remote(a.at[arow(owner, piece, y * quarter + t * piece)], av.at[g, 2 + s, qrow(y, t)],
                      ax_send, ax_recv.at[g, s, t], device)

    def a_near(g, s, t, d):
        ref = av.at[g, 2 + s, qrow(y, t)]
        recv = ay_recv.at[g, s, t] if d == s else ao_recv.at[g, max(t - 1, 0)]
        return remote(ref, ref, ay_send, recv, (up, down)[d])

    def a_far(g, s, t):
        ref = av.at[g, 2 + s, qrow((ym, yp)[s], t)]
        return remote(ref, ref, af_send, af_recv.at[g, max(t - 1, 0)], (up, down)[s])

    def a_first(g, s, t):
        a_cross(g, s, t).wait_recv()
        for d in range(2):
            a_near(g, s, t, d).start()

    def a_second(g, s, t):
        a_near(g, s, t, s).wait_recv()
        a_far(g, s, t).start()

    def group_arrival(sem, g, group):
        ref = av.at[g, 2, pl.ds(0, 2 * piece * (2 if group == 0 else 1))]
        return remote(ref, ref, ay_send, sem.at[g, group], part)

    def a_third(g, group):
        group_arrival(ao_recv, g, group).wait_recv()

    def a_fourth(g, group):
        group_arrival(af_recv, g, group).wait_recv()

    def w_part(j):
        return remote(w.at[:, wcol(j)], wbuf.at[0, j], wp_send, wp_recv.at[j], part)

    def w_cross(j):
        return remote(w.at[:, wcol(j)], wbuf.at[1, j], wa_send, wa_recv.at[j], acore)

    def w_pass(j):
        return remote(wbuf.at[1, j], wbuf.at[2, j], wf_send, wf_recv.at[j], part)

    def w_load(g, j, k):
        src = w.at[:, wcol(j)] if k == 0 else wbuf.at[k - 1, j]
        return pltpu.make_async_copy(src, wv.at[g, k], wl_sem.at[g, k])

    def w_loads(g, j):
        for k in range(4):
            w_load(g, j, k).start()

    def out_copy(j):
        slot = lax.rem(j, 2)
        return remote(ov.at[slot], hbuf.at[j], o_send.at[slot], o_recv.at[j], bcore)

    def quarter_of(k):
        return lax.rem(y + lax.div(k + 1, 2) * (2 * lax.rem(k, 2) - 1) + ny, ny)

    def out_rows(i):
        return pl.ds(pl.multiple_of(quarter_of(i) * quarter, 16), quarter)

    def out_part(j, rs):
        slot = lax.rem(j, 2)
        return remote(ov.at[slot, rs], hbuf.at[j, rs], o_send.at[slot], o_recv.at[j], bcore)

    def r_load(j):
        return pltpu.make_async_copy(r.at[:, wcol(j)], rv, r_sem)

    def block_product(lhs, rhs):
        return jnp.dot(lhs, rhs, preferred_element_type=jnp.float32).astype(jnp.bfloat16)

    def summed(g, buf, rs):
        acc = None
        for k in range(4):
            prod = block_product(av[g, k, rs, :], wv[buf, k]).astype(jnp.float32)
            acc = prod if acc is None else acc + prod
        return acc

    def in_parts(j):
        return (j == 2) | (j == 5) | (j == 8)

    def gemm_out(j):
        slot = lax.rem(j, 2)

        def step(i, carry):
            rs = out_rows(i)
            ov[slot, rs, :] = summed(0, 0, rs)

            @pl.when((i >= 1) & in_parts(j))
            def _():
                out_part(j, out_rows(i - 1)).start()

            return carry

        lax.fori_loop(0, ny, step, 0)

    def load_chunk(j, buf):
        with jax.named_scope("w_cross_wait"):
            w_cross(j).wait_recv()
        w_pass(j).start()
        w_load(buf, j, 0).start()
        w_load(buf, j, 2).start()
        with jax.named_scope("w_pass_wait"):
            w_part(j).wait_recv()
            w_load(buf, j, 1).start()
            w_pass(j).wait_recv()
            w_load(buf, j, 3).start()

    def load_wait(j, buf):
        with jax.named_scope("w_load_wait"):
            for k in range(4):
                w_load(buf, j, k).wait()

    most = (PIECES - 1) * ny

    def first_part(n):
        late = lax.div(n, 2 * most)
        early = 1 - late
        j = late * lax.rem(n, 2) + early * lax.div(n, most)
        t = late * (PIECES - 1) + early * lax.div(lax.rem(n, most), ny)
        k = late * lax.div(n - 2 * most, 2) + early * lax.rem(n, ny)
        return j, pl.ds(pl.multiple_of(quarter_of(k) * quarter + t * piece, 16), piece)

    def pass_on(t):
        for s in range(2):
            a_first(0, s, t)
        for s in range(2):
            a_second(0, s, t)
        a_third(0, t - 1)

    def first_chunks():
        def step(n, carry):
            @pl.when(n == ny - 1)
            def _():
                a_fourth(0, 0)

            @pl.when(n == 2 * ny)
            def _():
                with jax.named_scope("a0_piece2"):
                    pass_on(2)

            @pl.when(n == 3 * ny - 1)
            def _():
                with jax.named_scope("a0_far2"):
                    a_fourth(0, 1)

            @pl.when(n == most)
            def _():
                load_chunk(1, 1)
                load_wait(1, 1)

            @pl.when(n == 2 * most)
            def _():
                with jax.named_scope("a0_piece3"):
                    pass_on(3)

            @pl.when(n == 2 * most + 2 * ny - 2)
            def _():
                with jax.named_scope("a0_far3"):
                    a_fourth(0, 2)

            j, rs = first_part(n)
            ov[j, rs, :] = summed(0, j, rs)

            @pl.when(n >= 1)
            def _():
                out_part(*first_part(n - 1)).start()

            return carry

        lax.fori_loop(0, 2 * PIECES * ny, step, 0)
        out_part(*first_part(2 * PIECES * ny - 1)).start()

    def gemm_own(buf):
        def step(i, carry):
            rs = pl.ds(pl.multiple_of(i * tile, tile), tile)
            lv[rs, :] = summed(1, buf, rs)
            return carry

        lax.fori_loop(0, rows // tile, step, 0)

    items = ((xb, 0), (xb, 1), (xab, 0), (xab, 1), (x, o), (xa, o), (x, c), (xa, c))

    def at_load(n):
        pos, core = items[n]
        return pltpu.make_async_copy(a.at[arow(pos * CORES + core)], at.at[n % 2], at_sem.at[n % 2])

    def item_send(n):
        if n < 4:
            slot = n // 2 * 2 + c
            device = {"tp": xb * CORES + n % 2}
            return remote(pv.at[n], sb.at[slot], sb_send, sb_recv.at[slot], device)
        return remote(pv.at[n], sp.at[n - 4], sp_send, sp_recv.at[n - 4], part)

    def item(n):
        at_load(n).wait()

        def step(i, carry):
            rs = pl.ds(pl.multiple_of(i * tile, tile), tile)
            pv[n, rs, :] = block_product(at[n % 2, rs, :], wv[0, 0])
            return carry

        lax.fori_loop(0, rows // tile, step, 0)
        if n + 2 < len(items):
            at_load(n + 2).start()

    def sb_arrival(slot):
        return remote(pv.at[0], sb.at[slot], sb_send, sb_recv.at[slot], bcore)

    def sf_copy():
        return remote(sg, hbuf.at[last], sf_send, sf_recv, acore)

    def for_rows(body):
        def step(t, carry):
            body(pl.ds(pl.multiple_of(t * 64, 64), 64))
            return carry

        lax.fori_loop(0, rows // 64, step, 0)

    def finish(j, rs, h):
        hbuf[j, rs, :] = h
        sq = h * h
        acc = ssacc[rs, :]
        for l in range(CN // 128):
            acc = acc + sq[:, l * 128:(l + 1) * 128]
        ssacc[rs, :] = acc

    def wide(v):
        return v.astype(jnp.float32)

    barrier = pltpu.get_barrier_semaphore()
    peers = [part, acore, aother, bcore, bother] + [{"tp2": lax.rem(y + d, ny)} for d in range(1, ny)]
    for peer in peers:
        pl.semaphore_signal(barrier, inc=1, device_id=peer, device_id_type=MESH)
    w_last = pltpu.make_async_copy(w.at[:, wcol(last)], wv.at[0, 0], wl_sem.at[0, 0])
    w_last.start()
    at_load(0).start()
    at_load(1).start()
    pl.semaphore_wait(barrier, len(peers))

    for t in range(2):
        for s in range(2):
            a_cross(0, s, t).start()
    a_part(0).start()
    for j in range(FIRST):
        w_cross(j).start()
        w_part(j).start()
        if j < 2:
            for s in range(2):
                a_cross(0, s, j + 2).start()
        if j == 4:
            for t in range(PIECES):
                a_cross(1, 0, t).start()
        if j in (6, 7):
            for t in range(2):
                a_cross(1, 1, 2 * (j - 6) + t).start()
    a_part(1).start()
    w_last.wait()
    with jax.named_scope("items"):
        item(0)
        item(1)
        item_send(0).start()
        item(2)
        item_send(1).start()
        item(3)
        item_send(2).start()
    a_local(0).start()
    a_local(1).start()
    ssacc[...] = jnp.zeros_like(ssacc)
    item_send(3).start()
    with jax.named_scope("a0_first"):
        for t in range(2):
            for s in range(2):
                a_first(0, s, t)
    with jax.named_scope("items_2"):
        for n in range(4, 8):
            item(n)
        item_send(4).start()
        item_send(5).start()
    with jax.named_scope("a0_second"):
        for t in range(2):
            for s in range(2):
                a_second(0, s, t)
    with jax.named_scope("a0_third"):
        a_local(0).wait()
        a_part(0).wait_recv()
        a_third(0, 0)
    load_chunk(0, 0)
    load_wait(0, 0)
    with jax.named_scope("first_chunks"):
        first_chunks()

    def merge_last():
        r_load(last).start()
        sb_arrival(0).wait_recv()
        sb_arrival(1).wait_recv()
        with jax.named_scope("sf_wait"):
            sf_copy().wait_recv()
        r_load(last).wait()
        for_rows(lambda rs: finish(last, rs, wide(rv[rs, :]) + (
            (wide(pv[6, rs, :]) + wide(sp[0, rs, :])) + (wide(sb[0, rs, :]) + wide(sb[1, rs, :])) + hbuf[last, rs, :])))

    def sum_last():
        for n in range(2):
            item_send(4 + n).wait_recv()
            sb_arrival(2 + n).wait_recv()

        def body(rs):
            sg[rs, :] = (wide(pv[7, rs, :]) + wide(sp[1, rs, :])) + (wide(sb[2, rs, :]) + wide(sb[3, rs, :]))

        for_rows(body)

    def step(j, carry):
        @pl.when(j < last)
        def _():
            load_chunk(j, 0)

            @pl.when(j + AHEAD < last)
            def _():
                w_cross(j + AHEAD).start()
                w_part(j + AHEAD).start()

            with jax.named_scope("o_send_wait"):
                out_copy(j - 2).wait_send()
            load_wait(j, 0)
            with jax.named_scope("gemm0"):
                gemm_out(j)

            @pl.when(in_parts(j))
            def _():
                out_part(j, out_rows(ny - 1)).start()

            @pl.when(jnp.logical_not(in_parts(j)))
            def _():
                out_copy(j).start()

        @pl.when(j == LAG)
        def _():
            w_loads(1, 1)

        @pl.when((j >= LAG) & (2 * (j - LAG) < last))
        def _():
            w_loads(0, 2 * (j - LAG))

        @pl.when(j == 4)
        def _():
            with jax.named_scope("a1_4"):
                for t in range(PIECES):
                    a_first(1, 0, t)

        @pl.when(j == 5)
        def _():
            with jax.named_scope("a1_5"):
                for t in range(PIECES):
                    a_second(1, 0, t)

        @pl.when(j == LAG - 1)
        def _():
            with jax.named_scope("a1_6"):
                for t in range(2):
                    a_first(1, 1, t)
                for t in range(2):
                    a_second(1, 1, t)

        @pl.when(j == LAG)
        def _():
            with jax.named_scope("a1_7"):
                for t in range(2, PIECES):
                    a_first(1, 1, t)
                for t in range(2, PIECES):
                    a_second(1, 1, t)
                a_local(1).wait()
                a_part(1).wait_recv()
                for group in range(3):
                    a_third(1, group)
                    a_fourth(1, group)

        @pl.when(j == last - 3)
        def _():
            with jax.named_scope("sum_last"):
                sum_last()

        @pl.when(j == last)
        def _():
            with jax.named_scope("drain"):
                drain()

        @pl.when(j == last + 1)
        def _():
            with jax.named_scope("merge_last"):
                merge_last()

        def own(i, inner):
            buf = lax.rem(i, 2)
            r_load(i).start()
            with jax.named_scope("local_load_wait"):
                for k in range(4):
                    w_load(buf, i, k).wait()
            with jax.named_scope("gemm1"):
                gemm_own(buf)

            @pl.when((buf == 1) & (i + 2 < last))
            def _():
                w_loads(1, i + 2)

            r_load(i).wait()
            with jax.named_scope("o_recv_wait"):
                out_copy(i).wait_recv()
            with jax.named_scope("merge"):
                for_rows(lambda rs: finish(i, rs, wide(rv[rs, :]) + (lv[rs, :] + hbuf[i, rs, :])))
            return inner

        @pl.when(j >= LAG)
        def _():
            n = 2 * (j - LAG)
            lax.fori_loop(jnp.maximum(n - 1, 0), jnp.minimum(n + 1, last), own, 0)

        @pl.when(j == last - 3)
        def _():
            sf_copy().start()

        return carry

    def drain():
        def sent(ref, sem):
            remote(ref, ref, sem, sf_recv, part).wait_send()

        sent(wbuf.at[1], wa_send)
        sent(wbuf.at[0], wp_send)
        sent(wbuf.at[2], wf_send)
        sent(av.at[0, pl.ds(0, 2)], ap_send)
        sent(av.at[0, 0], ax_send)
        sent(av.at[0, pl.ds(0, 2)], ay_send)
        sent(av.at[0, 0], af_send)
        sent(sb, sb_send)
        sent(sp, sp_send)

    lax.fori_loop(2, LAG + (last + 1) // 2, step, 0)

    with jax.named_scope("sums"):
        full = lax.dot_general(jnp.ones((8, 128), jnp.float32), ssacc[...], (((1,), (1,)), ((), ())),
                               preferred_element_type=jnp.float32, precision=lax.Precision.HIGHEST)
        line = lax.broadcasted_iota(jnp.int32, (8, 128), 0)
        packed = jnp.zeros((8, 128), jnp.float32)
        for b in range(rows // 128):
            packed = jnp.where(line == b, full[:, b * 128:(b + 1) * 128], packed)
        svr[y] = packed
        sf_copy().wait_send()
        out_copy(last - 2).wait_send()
        out_copy(last - 1).wait_send()
    with jax.named_scope("sums_exchange"):
        sums = [remote(svr.at[y], svr.at[y], s_send, s_recv.at[d - 1], {"tp2": lax.rem(y + d, ny)})
                for d in range(1, ny)]
        for copy in sums:
            copy.start()
        for d in range(1, ny):
            src = lax.rem(y + ny - d, ny)
            remote(svr.at[src], svr.at[src], s_send, s_recv.at[d - 1], part).wait_recv()
        total = svr[0]
        for q in range(1, ny):
            total = total + svr[q]
        ssq_out[...] = total
        ref = svr.at[pl.ds(0, ny - 1)]
        remote(ref, ref, s_send, s_recv.at[0], part).wait_send()


def norm_kernel(width, h, ssq, gain, hidden, normed, scale, hs, ns, h_sem, n_sem):
    chunks, rows, cols = h.shape
    span = 64
    inv_rms = lax.rsqrt(ssq[...] / width + EPS_NORM)
    columns = jnp.transpose(inv_rms)
    for b in range(rows // 128):
        scale[b * 128:(b + 1) * 128, :] = jnp.broadcast_to(columns[:, b:b + 1], (128, scale.shape[1]))

    def block(t, carry):
        rs = pl.ds(pl.multiple_of(t * span, span), span)
        factor = scale[rs, :]
        for j in range(chunks):
            cs = slice(j * cols, (j + 1) * cols)
            value = h[j, rs, :]
            hs[rs, cs] = value.astype(jnp.bfloat16)
            ns[rs, cs] = (value * factor * gain[:, cs]).astype(jnp.bfloat16)
        pltpu.make_async_copy(hs.at[rs], hidden.at[rs], h_sem).start()
        pltpu.make_async_copy(ns.at[rs], normed.at[rs], n_sem).start()
        return carry

    lax.fori_loop(0, rows // span, block, 0)
    pltpu.make_async_copy(hs, hidden, h_sem).wait()
    pltpu.make_async_copy(ns, normed, n_sem).wait()


def solution(mesh):
    tp, ny = mesh.shape["tp"], mesh.shape["tp2"]
    chips = tp // CORES

    def local_step(a, w, r, gain):
        depth, cols = w.shape
        rows = r.shape[0]
        last = cols // CN - 1
        dma = pltpu.SemaphoreType.DMA
        any_space = pl.BlockSpec(memory_space=pl.ANY)
        bf16, f32 = jnp.bfloat16, jnp.float32
        chunks = last + 1
        vmem = pl.BlockSpec(memory_space=pltpu.VMEM)
        h, ssq, _ = pl.pallas_call(
            functools.partial(kernel, ny, chips),
            out_shape=(
                pltpu.VMEM((chunks, rows, CN), f32),
                pltpu.VMEM((8, 128), f32),
                jax.ShapeDtypeStruct((3, last, depth, CN), bf16),
            ),
            in_specs=[any_space] * 3,
            out_specs=(vmem, vmem, any_space),
            scratch_shapes=[
                pltpu.VMEM((2, 4, rows, depth), bf16),
                pltpu.VMEM((2, 4, depth, CN), bf16),
                pltpu.VMEM((2, rows, CN), f32),
                pltpu.VMEM((rows, CN), f32),
                pltpu.VMEM((rows, CN), bf16),
                pltpu.VMEM((rows, 128), f32),
                pltpu.VMEM((ny, 8, 128), f32),
                pltpu.VMEM((2, rows, depth), bf16),
                pltpu.VMEM((8, rows, CN), bf16),
                pltpu.VMEM((4, rows, CN), bf16),
                pltpu.VMEM((2, rows, CN), bf16),
                pltpu.VMEM((rows, CN), f32),
                dma((2,)), dma(()), dma((2,)), dma(()), dma((2, 2, PIECES)),
                dma(()), dma((2, 2, PIECES)), dma((2, 3)), dma(()), dma((2, 3)),
                dma(()), dma((last,)), dma(()), dma((last,)), dma(()), dma((last,)),
                dma((2,)), dma((last,)),
                dma((2, 4)), dma(()), dma(()), dma((ny - 1,)),
                dma((2,)), dma(()), dma((4,)), dma(()), dma((2,)), dma(()), dma(()),
            ],
            compiler_params=pltpu.CompilerParams(
                collective_id=0, has_side_effects=True, vmem_limit_bytes=54400000),
            cost_estimate=pl.CostEstimate(
                flops=2 * 8 * rows * depth * cols, bytes_accessed=8 * depth * cols * 2, transcendentals=0),
        )(a, w, r)
        return pl.pallas_call(
            functools.partial(norm_kernel, cols * ny),
            out_shape=(jax.ShapeDtypeStruct((rows, cols), bf16),) * 2,
            in_specs=[vmem] * 3,
            out_specs=(any_space, any_space),
            scratch_shapes=[
                pltpu.VMEM((rows, CN), f32), pltpu.VMEM((rows, cols), bf16), pltpu.VMEM((rows, cols), bf16),
                dma(()), dma(()),
            ],
            compiler_params=pltpu.CompilerParams(vmem_limit_bytes=24 << 20),
            cost_estimate=pl.CostEstimate(flops=4 * rows * cols, bytes_accessed=8 * rows * cols, transcendentals=rows),
        )(pltpu.with_memory_space_constraint(h, pltpu.VMEM), pltpu.with_memory_space_constraint(ssq, pltpu.VMEM), gain.reshape(1, cols))

    row_spec = P(("dp", "tp"), "tp2")
    return jax.shard_map(local_step, mesh=mesh, in_specs=(P("dp", "tp"), P("tp", "tp2"), row_spec, P("tp2")),
                         out_specs=(row_spec, row_spec), check_vma=False)
```

profile of v0, /device:TPU:96, one launch (start us, length us, event | category | flops | bytes accessed | tf_op | source)
XLA Modules:
  0.0 318.9 jit_solution(10028936242538363374)
XLA Ops:
  0.6 0.0 copy-start
  0.6 313.3 %shard_map.59 = (f32[12,1024,256]{2,1,0:T(8,128)S(1)}, f32[8,128]{1,0:T(8,128)S(1)}, bf16[3,11,1536,256]{3,2,1,0:T(8,128)(2,1)}) custom-call(bf16[8192,1536]{1,0:T(8,128)(2,1)} %a.1, bf16[1536,3072]{1,0:T(8,128)(2,1)} %w.1, bf16[1024,3072]{1,0:T(8,128)(2,1)} %r.1), custom_call_target="tpu_custom_call" | custom-call | flops 77309411328 | bytes 75497472 | tf_op jit(solution)/shard_map/pallas_call | solution.py:567
  313.9 0.0 copy-done
  313.9 5.0 %shard_map.60 = (bf16[1024,3072]{1,0:T(8,128)(2,1)}, bf16[1024,3072]{1,0:T(8,128)(2,1)}) custom-call(f32[12,1024,256]{2,1,0:T(8,128)S(1)} %get-tuple-element.4.h, f32[8,128]{1,0:T(8,128)S(1)} %get-tuple-element.5.ssq, f32[1,3072]{1,0:T(1,128)S(1)} %bitcast.1), custom_call_target="tpu_custom_call" | custom-call | flops 12582912 | bytes 25165824 | tf_op jit(solution)/shard_map/pallas_call | solution.py:601
Async XLA Ops:
  0.6 313.3 %copy-start = (f32[3072]{0:T(1024)S(1)}, f32[3072]{0:T(1024)}, u32[]{:S(2)}) copy-start(f32[3072]{0:T(1024)} %param.7) | copy-start | bytes 36868
where the time goes:
time: 320 us; the launch traced here: 319 us
  Pallas kernels  318 us (99%)
    pallas_call x1, Pallas kernels, local_step(): pl.pallas_call(functools.partial(kernel, ny, chips), out_shape=(pltpu.VME...  313 us

commit v1 on v0

--- a/solution.py
+++ b/solution.py
@@ -139,7 +139,7 @@
         return acc
 
     def in_parts(j):
-        return (j == 2) | (j == 5) | (j == 8)
+        return j <= 8
 
     def gemm_out(j):
         slot = lax.rem(j, 2)

time: 320 us -> 320 us (level)
  no operation moved by 1% of the time
where the time goes in v1:
time: 320 us; the launch traced here: 319 us
  Pallas kernels  318 us (99%)
    pallas_call x1, Pallas kernels, local_step(): pl.pallas_call(functools.partial(kernel, ny, chips), out_shape=(pltpu.VME...  313 us

profile of v1, /device:TPU:96, one launch (start us, length us, event | category | flops | bytes accessed | tf_op | source)
XLA Modules:
  0.0 318.9 jit_solution(17000885934933974203)
XLA Ops:
  0.6 0.0 copy-start
  0.6 313.3 %shard_map.59 = (f32[12,1024,256]{2,1,0:T(8,128)S(1)}, f32[8,128]{1,0:T(8,128)S(1)}, bf16[3,11,1536,256]{3,2,1,0:T(8,128)(2,1)}) custom-call(bf16[8192,1536]{1,0:T(8,128)(2,1)} %a.1, bf16[1536,3072]{1,0:T(8,128)(2,1)} %w.1, bf16[1024,3072]{1,0:T(8,128)(2,1)} %r.1), custom_call_target="tpu_custom_call" | custom-call | flops 77309411328 | bytes 75497472 | tf_op jit(solution)/shard_map/pallas_call | solution.py:567
  313.9 0.0 copy-done
  313.9 5.0 %shard_map.60 = (bf16[1024,3072]{1,0:T(8,128)(2,1)}, bf16[1024,3072]{1,0:T(8,128)(2,1)}) custom-call(f32[12,1024,256]{2,1,0:T(8,128)S(1)} %get-tuple-element.4.h, f32[8,128]{1,0:T(8,128)S(1)} %get-tuple-element.5.ssq, f32[1,3072]{1,0:T(1,128)S(1)} %bitcast.1), custom_call_target="tpu_custom_call" | custom-call | flops 12582912 | bytes 25165824 | tf_op jit(solution)/shard_map/pallas_call | solution.py:601
Async XLA Ops:
  0.6 313.3 %copy-start = (f32[3072]{0:T(1024)S(1)}, f32[3072]{0:T(1024)}, u32[]{:S(2)}) copy-start(f32[3072]{0:T(1024)} %param.7) | copy-start | bytes 36868
